TPU v7x, 32 devices: a whole 2x2x4 slice. The times are simulated.
32 devices in a mesh: mem: 4 (over y, x), cell: 8 (over z, core).
Axes of the slice: x: 2, y: 2, z: 4, core: 2. Of those that a mesh axis runs over, the one named last changes fastest.
Arguments:
- state: bfloat16 [16384, 40, 120], P('cell', 'mem'), may hold values from -6 to 6
- vertical_weight: bfloat16 [8192, 120], P('cell'), may hold values from -0.5 to 0.5
- horizontal_weight: float32 [8192, 4], P('cell'), may hold values from 0.05 to 0.45
- obs_slot: int32 [8192, 4], P('cell'), may hold values from 0 to 4095, as said below
- request_cell: int32 [8, 4096], P('cell'), may hold values from 0 to 2047
- obs_value: float32 [8192], P('cell'), may hold values from -6 to 6
- obs_error: float32 [8192], P('cell'), may hold values from 0.5 to 2
- obs_region: int32 [8192], P('cell'), may hold values from 0 to 63, as said below
Outputs:
- cov_matrix: float32 [64, 40, 40], P('cell', 'mem')
- innovation_proj: float32 [64, 40], P('cell', 'mem')
Inputs may be any that keep to these rules, and one draw needn't show every extreme that they name: `obs_slot`: within one owner's 1024 observations all 4096 slots differ, so every slot is used: 1024 ask the owner's own patch and 768 each of the four patches at distance 1 and 2. `obs_region`: an observation's region is one of the 8 regions of its owner's patch or of the patches just before or after it (indices wrap); patch p holds regions p * 8 to p * 8 + 7.
All inputs are finite; a program needn't handle non-finite values.
Results may differ from a plain program's by a relative error of at most 0.0003.
Values may be sent and summed in bfloat16 or wider, within the bound.
A program may use at most 128 MiB of HBM per device.

v0:
```python
import jax
import jax.numpy as jnp
from jax import lax
from jax.sharding import PartitionSpec as P

REG_DEV = 8


halo_moves = (-2, -1, 1, 2)


def passed_along(x, axis, by):
    devices = lax.axis_size(axis)
    return lax.ppermute(x, axis, [(i, (i + by) % devices) for i in range(devices)])


def ask_patch(wanted_cells, offset):
    return passed_along(wanted_cells, "cell", offset)


def on_device(
    state,
    vertical_weight,
    horizontal_weight,
    obs_slot,
    request_cell,
    obs_value,
    obs_error,
    obs_region,
):
    patches = lax.axis_size("cell")
    here = lax.axis_index("cell")
    cell_dev, mem_dev, levels = state.shape
    obs_dev, neigh = obs_slot.shape
    halo_cap = 3 * obs_dev // 4
    total_slots = 4 * obs_dev
    flat_state = state.reshape(cell_dev, mem_dev * levels)
    flat_slot = obs_slot.reshape(-1)
    table = request_cell.reshape(-1)
    slot_ids = lax.iota(jnp.int32, total_slots)
    inverse_slot = jnp.zeros((total_slots,), jnp.int32).at[flat_slot].set(slot_ids)
    slot_obs = inverse_slot // neigh
    slot_hweight = jnp.take(horizontal_weight.reshape(-1), inverse_slot, axis=0)
    slot_vweight = jnp.take(vertical_weight, slot_obs, axis=0)
    own_cols = jnp.take(flat_state, table[:obs_dev], axis=0).reshape(obs_dev, mem_dev, levels)
    pieces = []
    pieces.append(
        jnp.einsum(
            "rml,rl->mr", own_cols, slot_vweight[:obs_dev], preferred_element_type=jnp.float32
        )
    )
    for number, offset in enumerate(halo_moves):
        lower = obs_dev + number * halo_cap
        wanted = ask_patch(table[lower : lower + halo_cap], offset)
        incoming = passed_along(slot_vweight[lower : lower + halo_cap], "cell", offset)
        picked_cols = jnp.take(flat_state, wanted, axis=0).reshape(halo_cap, mem_dev, levels)
        at_patch = jnp.einsum(
            "rml,rl->mr", picked_cols, incoming, preferred_element_type=jnp.float32
        )
        pieces.append(passed_along(at_patch, "cell", -offset))
    equiv = jnp.concatenate(pieces, axis=1)
    obs_ids = lax.iota(jnp.int32, obs_dev)
    mixing = (slot_obs[:, None] == obs_ids[None, :]).astype(jnp.float32) * slot_hweight[:, None]
    own_equiv = jnp.dot(
        equiv, mixing, precision=lax.Precision.HIGHEST, preferred_element_type=jnp.float32
    )
    everyone = lax.all_gather(own_equiv, "mem", axis=0, tiled=True)
    mean = jnp.mean(everyone, axis=0, keepdims=True)
    spread_all = everyone - mean
    spread_own = own_equiv - mean
    members = everyone.shape[0]
    inverse = 1.0 / (obs_error * obs_error)
    innov = (obs_value - mean[0]) * inverse
    reg_dev = REG_DEV
    relative = jnp.mod(obs_region - (here - 1) * reg_dev, patches * reg_dev)
    region_ids = lax.iota(jnp.int32, 3 * reg_dev)
    onehot = (region_ids[:, None] == relative[None, :]).astype(jnp.float32)
    masked = (onehot[:, None, :] * spread_own[None, :, :]).reshape(3 * reg_dev * mem_dev, obs_dev)
    scaled_all = spread_all * inverse[None, :]
    cov_part = lax.dot_general(
        masked,
        scaled_all,
        (((1,), (1,)), ((), ())),
        precision=lax.Precision.HIGHEST,
        preferred_element_type=jnp.float32,
    )
    vec_part = jnp.dot(
        masked, innov, precision=lax.Precision.HIGHEST, preferred_element_type=jnp.float32
    )
    sums = jnp.concatenate(
        [cov_part.reshape(3 * reg_dev, mem_dev * members), vec_part.reshape(3 * reg_dev, mem_dev)],
        axis=1,
    )
    from_prev = passed_along(sums[2 * reg_dev :], "cell", 1)
    from_next = passed_along(sums[:reg_dev], "cell", -1)
    summed = sums[reg_dev : 2 * reg_dev] + from_prev + from_next
    cov_matrix = summed[:, : mem_dev * members].reshape(reg_dev, mem_dev, members)
    innovation_proj = summed[:, mem_dev * members :]
    return (cov_matrix, innovation_proj)


def solution(mesh):
    in_specs = (
        P("cell", "mem", None),
        P("cell", None),
        P("cell", None),
        P("cell", None),
        P("cell", None),
        P("cell"),
        P("cell"),
        P("cell"),
    )
    out_specs = (P("cell", "mem", None), P("cell", "mem"))
    return jax.shard_map(
        on_device, mesh=mesh, in_specs=in_specs, out_specs=out_specs, check_vma=False
    )
```

profile of v0, /device:TPU:0, one launch (start us, length us, event | category | flops | bytes accessed | tf_op | source)
XLA Modules:
  0.0 193.7 jit_solution(2439177249630479289)
XLA Ops:
  0.6 0.8 slice_reduce_fusion
  1.4 3.1 %collective-permute-start.10 = (s32[768]{0:T(1024)S(1)}, s32[768]{0:T(1024)S(1)}, u32[]{:S(2)}, u32[]{:S(2)}) collective-permute-start(s32[768]{0:T(1024)S(1)} %get-tuple-element.7), channel_id=1, source_target_pairs={{0,2},{1,3},{2,4},{3,5},{4,6},{5,7},{6,0},{7,1},{8,10},{9,11},{10,... | collective-permute-start | bytes 9224 | tf_op jit(solution)/shard_map/ppermute | solution.py:14
  4.5 1.5 collective-permute-start.4
  6.0 1.7 collective-permute-start.1
  7.7 1.1 copy.28
  8.8 0.9 copy.27
  10.2 15.5 %scatter_custom_fusion = s32[4096]{0:T(1024)S(1)} fusion(s32[4096]{0:T(1024)S(1)} %bitcast.55, s32[4096]{0:T(1024)S(1)} %iota.14, s32[]{:T(128)} %constant.85.clone.1), kind=kCustom, calls=%fused_computation.70 | custom fusion | bytes 16388 | tf_op jit(solution)/shard_map/scatter | solution.py:41
  25.7 12.1 %gather_fusion = bf16[4096,120]{1,0:T(8,128)(2,1)S(1)} fusion(bf16[1024,120]{1,0:T(8,128)(2,1)S(1)} %copy.28, s32[4096]{0:T(1024)S(1)} %get-tuple-element.23), kind=kCustom, calls=%fused_computation.4 | custom fusion | bytes 1982464 | tf_op jit(solution)/shard_map/jit(_take)/gather | solution.py:44
  37.9 2.1 %broadcast_select_fusion.4 = bf16[4096,120]{1,0:T(8,128)(2,1)S(1)} fusion(bf16[4096,120]{1,0:T(8,128)(2,1)S(1)} %gather_fusion, pred[4096]{0:T(1024)(128)(4,1)S(1)} %get-tuple-element.11), kind=kLoop, calls=%fused_computation.23 | loop fusion | flops 491520 | bytes 1970176 | tf_op jit(solution)/shard_map/jit(_take)/select_n | solution.py:44
  40.1 0.8 fusion.25
  42.1 7.8 %copy.29 = bf16[2048,1200]{1,0:T(8,128)(2,1)} copy(bf16[2048,1200]{0,1:T(8,128)(2,1)} %bitcast.44) | data formatting | bytes 9830400 | tf_op jit(solution)/shard_map/reshape | solution.py:37
  49.9 9.0 %gather_fusion.1 = bf16[1024,1200]{1,0:T(8,128)(2,1)S(1)} fusion(bf16[2048,1200]{1,0:T(8,128)(2,1)} %copy.29, s32[1024]{0:T(1024)S(1)} %broadcast_clamp_fusion), kind=kCustom, calls=%fused_computation.5 | custom fusion | bytes 4919296 | tf_op jit(solution)/shard_map/jit(_take)/gather | solution.py:45
  58.8 2.7 %copy.30 = bf16[1024,1200]{0,1:T(8,128)(2,1)} copy(bf16[1024,1200]{1,0:T(8,128)(2,1)S(1)} %gather_fusion.1) | data formatting | bytes 4915200 | tf_op jit(solution)/shard_map/jit(_take)/gather | solution.py:45
  61.5 2.4 %multiply_reduce_fusion = f32[1024,10]{0,1:T(8,128)S(1)} fusion(f32[1024,120]{0,1:T(8,128)S(1)} %copy.79, bf16[1024,10,120]{0,2,1:T(8,128)(2,1)} %bitcast.39, pred[1024]{0:T(1024)(128)(4,1)S(1)} %compare_and_fusion.5), kind=kLoop, calls=%fused_computation.14 | loop fusion | flops 4904960 | bytes 2991104 | tf_op jit(solution)/shard_map/rml,rl->mr/dot_general | solution.py:48
  63.9 0.6 bitcast_dynamic-update-slice_fusion
  64.6 23.0 %gather_fusion.2 = f32[4096]{0:T(1024)S(1)} fusion(f32[4096]{0:T(1024)S(1)} %reshape.159, s32[4096]{0:T(1024)S(1)} %get-tuple-element.22), kind=kCustom, calls=%fused_computation.6 | custom fusion | bytes 49152 | tf_op jit(solution)/shard_map/jit(_take)/gather | solution.py:43
  87.8 3.4 %collective-permute-start.3 = (bf16[768,120]{1,0:T(8,128)(2,1)S(1)}, bf16[768,120]{1,0:T(8,128)(2,1)S(1)}, u32[]{:S(2)}, u32[]{:S(2)}) collective-permute-start(bf16[768,120]{1,0:T(8,128)(2,1)S(1)} %get-tuple-element.15), channel_id=1, source_target_pairs={{0,7},{1,0},{2,1},{3,2},{4,3},{5,4},{6,5},{7,6},{8,15},{9,8},{10,9... | collective-permute-start | bytes 552968 | tf_op jit(solution)/shard_map/ppermute | solution.py:14
  91.3 1.9 collective-permute-start
  93.2 8.3 %gather_fusion.6 = bf16[768,1200]{1,0:T(8,128)(2,1)} fusion(bf16[2048,1200]{1,0:T(8,128)(2,1)} %copy.29, s32[1024]{0:T(1024)S(1)} %get-tuple-element.24), kind=kCustom, calls=%fused_computation.3.clone | custom fusion | bytes 3689472 | tf_op jit(solution)/shard_map/jit(_take)/gather | solution.py:56
  101.5 7.6 %gather_fusion.5 = bf16[768,1200]{1,0:T(8,128)(2,1)S(1)} fusion(bf16[2048,1200]{1,0:T(8,128)(2,1)} %copy.29, s32[1024]{0:T(1024)S(1)} %get-tuple-element.25), kind=kCustom, calls=%fused_computation.2.clone | custom fusion | bytes 3689472 | tf_op jit(solution)/shard_map/jit(_take)/gather | solution.py:56
  109.1 8.4 %gather_fusion.4 = bf16[768,1200]{1,0:T(8,128)(2,1)} fusion(bf16[2048,1200]{1,0:T(8,128)(2,1)} %copy.29, s32[1024]{0:T(1024)S(1)} %get-tuple-element.26), kind=kCustom, calls=%fused_computation.1.clone | custom fusion | bytes 3689472 | tf_op jit(solution)/shard_map/jit(_take)/gather | solution.py:56
  117.5 8.3 %gather_fusion.3 = bf16[768,1200]{1,0:T(8,128)(2,1)} fusion(bf16[2048,1200]{1,0:T(8,128)(2,1)} %copy.29, s32[1024]{0:T(1024)S(1)} %get-tuple-element.27), kind=kCustom, calls=%fused_computation.clone | custom fusion | bytes 3689472 | tf_op jit(solution)/shard_map/jit(_take)/gather | solution.py:56
  125.9 3.1 %broadcast_select_fusion = bf16[768,1200]{1,0:T(8,128)(2,1)} fusion(bf16[768,1200]{1,0:T(8,128)(2,1)} %gather_fusion.6, pred[768]{0:T(1024)(128)(4,1)S(1)} %compare_and_fusion.1), kind=kLoop, calls=%fused_computation.19 | loop fusion | flops 921600 | bytes 3687168 | tf_op jit(solution)/shard_map/jit(_take)/select_n | solution.py:56
  129.0 1.5 broadcast_select_fusion.1
  130.5 0.7 copy-done.1
  131.2 1.6 broadcast_select_fusion.2
  132.8 0.6 copy-done
  133.5 1.6 broadcast_select_fusion.3
  135.0 0.7 copy-done.2
  135.7 2.5 %copy.78 = bf16[768,1200]{0,1:T(8,128)(2,1)} copy(bf16[768,1200]{1,0:T(8,128)(2,1)S(1)} %copy-done.2) | data formatting | bytes 3686400
  138.2 4.2 %copy.77 = bf16[768,1200]{0,1:T(8,128)(2,1)} copy(bf16[768,1200]{1,0:T(8,128)(2,1)} %broadcast_select_fusion.1) | data formatting | bytes 3686400
  142.4 2.4 %copy.76 = bf16[768,1200]{0,1:T(8,128)(2,1)} copy(bf16[768,1200]{1,0:T(8,128)(2,1)S(1)} %copy-done.3) | data formatting | bytes 3686400
  144.7 4.0 %copy.75 = bf16[768,1200]{0,1:T(8,128)(2,1)} copy(bf16[768,1200]{1,0:T(8,128)(2,1)} %broadcast_select_fusion.3) | data formatting | bytes 3686400
  148.7 1.2 copy.83
  149.9 1.9 multiply_reduce_fusion.1
  152.9 1.2 copy.80
  154.1 1.9 multiply_reduce_fusion.4
  156.1 1.9 %collective-permute-start.2 = (f32[10,768]{1,0:T(8,128)S(1)}, f32[10,768]{1,0:T(8,128)S(1)}, u32[]{:S(2)}, u32[]{:S(2)}) collective-permute-start(f32[10,768]{1,0:T(8,128)S(1)} %bitcast.51), channel_id=1, source_target_pairs={{0,2},{1,3},{2,4},{3,5},{4,6},{5,7},{6,0},{7,1},{8,10},{9,11},{10,... | collective-permute-start | bytes 92168 | tf_op jit(solution)/shard_map/ppermute | solution.py:14
  158.7 3.3 %collective-permute-done.2 = f32[10,768]{1,0:T(8,128)S(1)} collective-permute-done((f32[10,768]{1,0:T(8,128)S(1)}, f32[10,768]{1,0:T(8,128)S(1)}, u32[]{:S(2)}, u32[]{:S(2)}) %collective-permute-start.2) | collective-permute-done | bytes 30752 | tf_op jit(solution)/shard_map/ppermute | solution.py:14
  162.0 1.9 %collective-permute-done.5 = f32[10,768]{1,0:T(8,128)S(1)} collective-permute-done((f32[10,768]{1,0:T(8,128)S(1)}, f32[10,768]{1,0:T(8,128)S(1)}, u32[]{:S(2)}, u32[]{:S(2)}) %collective-permute-start.5) | collective-permute-done | bytes 30752 | tf_op jit(solution)/shard_map/ppermute | solution.py:14
  164.0 9.5 %fusion = f32[10,1024]{1,0:T(8,128)S(1)} fusion(f32[10,4096]{1,0:T(8,128)S(1)} %constant_dynamic-update-slice_fusion, f32[4096]{0:T(1024)S(1)} %and_select_fusion, s32[4096]{0:T(1024)S(1)} %get-tuple-element.12), kind=kOutput, calls=%fused_computation.8 | convolution fusion | flops 511705088 | bytes 237568 | tf_op jit(solution)/shard_map/dot_general | solution.py:64
  173.5 9.2 %all-gather = f32[4,10,1024]{2,1,0:T(8,128)S(1)} all-gather(f32[1,10,1024]{2,1,0:T(8,128)S(1)} %bitcast.45), channel_id=1, replica_groups=mesh['mem'=4,'cell'=8] {'mem'}, dimensions={0}, use_global_device_ids=true | all-gather | bytes 204800 | tf_op jit(solution)/shard_map/all_gather | solution.py:67
  183.2 2.7 %fusion.5 = f32[1,24,10]{1,0,2:T(1,128)S(1)} fusion(f32[1024,1,1]{0,1,2:T(1,128)S(1)} %bitcast.54, f32[24,10,1024]{2,1,0:T(8,128)S(1)} %broadcast_multiply_fusion), kind=kOutput, calls=%fused_computation.24 | convolution fusion | flops 2949120 | bytes 988096 | tf_op jit(solution)/shard_map/dot_general | solution.py:87
  186.0 1.0 fusion.7
  187.2 3.5 %collective-permute-start.13 = (f32[8,410]{1,0:T(8,128)S(1)}, f32[8,410]{1,0:T(8,128)S(1)}, u32[]{:S(2)}, u32[]{:S(2)}) collective-permute-start(f32[8,410]{1,0:T(8,128)S(1)} %get-tuple-element.18), channel_id=1, source_target_pairs={{0,7},{1,0},{2,1},{3,2},{4,3},{5,4},{6,5},{7,6},{8,15},{9,8},{10,9... | collective-permute-start | bytes 39368 | tf_op jit(solution)/shard_map/ppermute | solution.py:14
  190.8 1.4 collective-permute-done.12
  192.3 0.7 slice.107
  193.0 0.6 copy.41
  (89 shorter events, 4.4 us)
Async XLA Ops:
  1.4 86.2 %collective-permute-start.10 = (s32[768]{0:T(1024)S(1)}, s32[768]{0:T(1024)S(1)}, u32[]{:S(2)}, u32[]{:S(2)}) collective-permute-start(s32[768]{0:T(1024)S(1)} %get-tuple-element.7), channel_id=1, source_target_pairs={{0,2},{1,3},{2,4},{3,5},{4,6},{5,7},{6,0},{7,1},{8,10},{9,11},{10,... | collective-permute-start | bytes 9224 | tf_op jit(solution)/shard_map/ppermute | solution.py:14
  4.5 83.3 %collective-permute-start.4 = (s32[768]{0:T(1024)S(1)}, s32[768]{0:T(1024)S(1)}, u32[]{:S(2)}, u32[]{:S(2)}) collective-permute-start(s32[768]{0:T(1024)S(1)} %get-tuple-element.8), channel_id=1, source_target_pairs={{0,7},{1,0},{2,1},{3,2},{4,3},{5,4},{6,5},{7,6},{8,15},{9,8},{10,9... | collective-permute-start | bytes 9224 | tf_op jit(solution)/shard_map/ppermute | solution.py:14
  6.0 103.1 %collective-permute-start.1 = (s32[768]{0:T(1024)S(1)}, s32[768]{0:T(1024)S(1)}, u32[]{:S(2)}, u32[]{:S(2)}) collective-permute-start(s32[768]{0:T(1024)S(1)} %get-tuple-element.9), channel_id=1, source_target_pairs={{0,6},{1,7},{2,0},{3,1},{4,2},{5,3},{6,4},{7,5},{8,14},{9,15},{10,... | collective-permute-start | bytes 9224 | tf_op jit(solution)/shard_map/ppermute | solution.py:14
  7.7 83.5 %collective-permute-start.7 = (s32[768]{0:T(1024)S(1)}, s32[768]{0:T(1024)S(1)}, u32[]{:S(2)}, u32[]{:S(2)}) collective-permute-start(s32[768]{0:T(1024)S(1)} %get-tuple-element.10), channel_id=1, source_target_pairs={{0,1},{1,2},{2,3},{3,4},{4,5},{5,6},{6,7},{7,0},{8,9},{9,10},{10,1... | collective-permute-start | bytes 9224 | tf_op jit(solution)/shard_map/ppermute | solution.py:14
  37.9 3.4 %copy-start.8 = (s32[1,4096]{1,0:T(1,128)S(1)}, s32[1,4096]{1,0:T(1,128)}, u32[]{:S(2)}) copy-start(s32[1,4096]{1,0:T(1,128)} %param.14) | copy-start | bytes 49156
  37.9 3.4 %slice-start = ((s32[1,4096]{1,0:T(1,128)}), s32[1,1024]{1,0:T(1,128)S(1)}, s32[]{:S(2)}) async-start(s32[1,4096]{1,0:T(1,128)} %param.14), calls=%async_computation | async-start | bytes 8192 | tf_op jit(solution)/shard_map/slice | solution.py:45
  37.9 3.5 %copy-start.11 = (s32[1024]{0:T(1024)S(1)}, s32[1024]{0:T(1024)}, u32[]{:S(2)}) copy-start(s32[1024]{0:T(1024)} %param.17) | copy-start | bytes 12292
  37.9 3.5 %copy-start.9 = (f32[1024,4]{0,1:T(4,128)S(1)}, f32[1024,4]{0,1:T(4,128)}, u32[]{:S(2)}) copy-start(f32[1024,4]{0,1:T(4,128)} %param.12) | copy-start | bytes 49156
  40.9 107.8 %collective-permute-start.9 = (bf16[768,120]{1,0:T(8,128)(2,1)}, bf16[768,120]{1,0:T(8,128)(2,1)}, u32[]{:S(2)}, u32[]{:S(2)}) collective-permute-start(bf16[768,120]{1,0:T(8,128)(2,1)} %get-tuple-element.13), channel_id=1, source_target_pairs={{0,2},{1,3},{2,4},{3,5},{4,6},{5,7},{6,0},{7,1},{8,10},{9,11},{10,... | collective-permute-start | bytes 552968 | tf_op jit(solution)/shard_map/ppermute | solution.py:14
  64.6 23.1 %copy-start.7 = (bf16[768,120]{1,0:T(8,128)(2,1)S(1)}, bf16[768,120]{1,0:T(8,128)(2,1)}, u32[]{:S(2)}) copy-start(bf16[768,120]{1,0:T(8,128)(2,1)} %get-tuple-element.14) | copy-start | bytes 552964
  64.6 26.7 %copy-start.6 = (bf16[768,120]{1,0:T(8,128)(2,1)S(1)}, bf16[768,120]{1,0:T(8,128)(2,1)}, u32[]{:S(2)}) copy-start(bf16[768,120]{1,0:T(8,128)(2,1)} %get-tuple-element.16) | copy-start | bytes 552964
  87.6 64.4 %collective-permute-start.6 = (bf16[768,120]{1,0:T(8,128)(2,1)S(1)}, bf16[768,120]{1,0:T(8,128)(2,1)S(1)}, u32[]{:S(2)}, u32[]{:S(2)}) collective-permute-start(bf16[768,120]{1,0:T(8,128)(2,1)S(1)} %copy-done.7), channel_id=1, source_target_pairs={{0,1},{1,2},{2,3},{3,4},{4,5},{5,6},{6,7},{7,0},{8,9},{9,10},{10,1... | collective-permute-start | bytes 552968 | tf_op jit(solution)/shard_map/ppermute | solution.py:14
  87.8 70.2 %collective-permute-start.3 = (bf16[768,120]{1,0:T(8,128)(2,1)S(1)}, bf16[768,120]{1,0:T(8,128)(2,1)S(1)}, u32[]{:S(2)}, u32[]{:S(2)}) collective-permute-start(bf16[768,120]{1,0:T(8,128)(2,1)S(1)} %get-tuple-element.15), channel_id=1, source_target_pairs={{0,7},{1,0},{2,1},{3,2},{4,3},{5,4},{6,5},{7,6},{8,15},{9,8},{10,9... | collective-permute-start | bytes 552968 | tf_op jit(solution)/shard_map/ppermute | solution.py:14
  91.3 61.6 %collective-permute-start = (bf16[768,120]{1,0:T(8,128)(2,1)S(1)}, bf16[768,120]{1,0:T(8,128)(2,1)}, u32[]{:S(2)}, u32[]{:S(2)}) collective-permute-start(bf16[768,120]{1,0:T(8,128)(2,1)S(1)} %copy-done.6), channel_id=1, source_target_pairs={{0,6},{1,7},{2,0},{3,1},{4,2},{5,3},{6,4},{7,5},{8,14},{9,15},{10,... | collective-permute-start | bytes 552968 | tf_op jit(solution)/shard_map/ppermute | solution.py:14
  129.0 2.3 %copy-start.1 = (bf16[768,1200]{1,0:T(8,128)(2,1)S(1)}, bf16[768,1200]{1,0:T(8,128)(2,1)}, u32[]{:S(2)}) copy-start(bf16[768,1200]{1,0:T(8,128)(2,1)} %gather_fusion.4) | copy-start | bytes 5529604
  131.2 2.3 %copy-start = (bf16[768,1200]{1,0:T(8,128)(2,1)S(1)}, bf16[768,1200]{1,0:T(8,128)(2,1)}, u32[]{:S(2)}) copy-start(bf16[768,1200]{1,0:T(8,128)(2,1)} %gather_fusion.3) | copy-start | bytes 5529604
  133.5 2.3 %copy-start.2 = (bf16[768,1200]{1,0:T(8,128)(2,1)S(1)}, bf16[768,1200]{1,0:T(8,128)(2,1)}, u32[]{:S(2)}) copy-start(bf16[768,1200]{1,0:T(8,128)(2,1)} %broadcast_select_fusion) | copy-start | bytes 5529604
  138.2 4.2 %copy-start.3 = (bf16[768,1200]{1,0:T(8,128)(2,1)S(1)}, bf16[768,1200]{1,0:T(8,128)(2,1)}, u32[]{:S(2)}) copy-start(bf16[768,1200]{1,0:T(8,128)(2,1)} %broadcast_select_fusion.2) | copy-start | bytes 5529604
  148.7 3.5 %copy-start.5 = (bf16[768,1200]{0,1:T(8,128)(2,1)S(1)}, bf16[768,1200]{0,1:T(8,128)(2,1)}, u32[]{:S(2)}) copy-start(bf16[768,1200]{0,1:T(8,128)(2,1)} %copy.77) | copy-start | bytes 5529604
  151.8 12.2 %collective-permute-start.11 = (f32[10,768]{1,0:T(8,128)S(1)}, f32[10,768]{1,0:T(8,128)S(1)}, u32[]{:S(2)}, u32[]{:S(2)}) collective-permute-start(f32[10,768]{1,0:T(8,128)S(1)} %bitcast.49), channel_id=1, source_target_pairs={{0,6},{1,7},{2,0},{3,1},{4,2},{5,3},{6,4},{7,5},{8,14},{9,15},{10,... | collective-permute-start | bytes 92168 | tf_op jit(solution)/shard_map/ppermute | solution.py:14
  152.6 5.6 %copy-start.4 = (bf16[768,1200]{0,1:T(8,128)(2,1)S(1)}, bf16[768,1200]{0,1:T(8,128)(2,1)}, u32[]{:S(2)}) copy-start(bf16[768,1200]{0,1:T(8,128)(2,1)} %copy.76) | copy-start | bytes 5529604
  152.6 11.4 %collective-permute-start.8 = (f32[10,768]{1,0:T(8,128)S(1)}, f32[10,768]{1,0:T(8,128)S(1)}, u32[]{:S(2)}, u32[]{:S(2)}) collective-permute-start(f32[10,768]{1,0:T(8,128)S(1)} %bitcast.50), channel_id=1, source_target_pairs={{0,7},{1,0},{2,1},{3,2},{4,3},{5,4},{6,5},{7,6},{8,15},{9,8},{10,9... | collective-permute-start | bytes 92168 | tf_op jit(solution)/shard_map/ppermute | solution.py:14
  156.1 6.0 %copy-start.10 = (f32[10,4096]{1,0:T(8,128)S(1)}, f32[10,4096]{1,0:T(8,128)}, u32[]{:S(2)}) copy-start(f32[10,4096]{1,0:T(8,128)} %bitcast_dynamic-update-slice_fusion) | copy-start | bytes 491524
  156.1 5.9 %collective-permute-start.2 = (f32[10,768]{1,0:T(8,128)S(1)}, f32[10,768]{1,0:T(8,128)S(1)}, u32[]{:S(2)}, u32[]{:S(2)}) collective-permute-start(f32[10,768]{1,0:T(8,128)S(1)} %bitcast.51), channel_id=1, source_target_pairs={{0,2},{1,3},{2,4},{3,5},{4,6},{5,7},{6,0},{7,1},{8,10},{9,11},{10,... | collective-permute-start | bytes 92168 | tf_op jit(solution)/shard_map/ppermute | solution.py:14
  158.6 5.4 %collective-permute-start.5 = (f32[10,768]{1,0:T(8,128)S(1)}, f32[10,768]{1,0:T(8,128)S(1)}, u32[]{:S(2)}, u32[]{:S(2)}) collective-permute-start(f32[10,768]{1,0:T(8,128)S(1)} %bitcast.52), channel_id=1, source_target_pairs={{0,1},{1,2},{2,3},{3,4},{4,5},{5,6},{6,7},{7,0},{8,9},{9,10},{10,1... | collective-permute-start | bytes 92168 | tf_op jit(solution)/shard_map/ppermute | solution.py:14
  164.0 18.8 %copy-start.12 = (f32[1024]{0:T(1024)S(1)}, f32[1024]{0:T(1024)}, u32[]{:S(2)}) copy-start(f32[1024]{0:T(1024)} %param.16) | copy-start | bytes 12292
  164.0 18.8 %copy-start.13 = (f32[1024]{0:T(1024)S(1)}, f32[1024]{0:T(1024)}, u32[]{:S(2)}) copy-start(f32[1024]{0:T(1024)} %param.15) | copy-start | bytes 12292
  187.2 5.0 %collective-permute-start.12 = (f32[8,410]{1,0:T(8,128)S(1)}, f32[8,410]{1,0:T(8,128)S(1)}, u32[]{:S(2)}, u32[]{:S(2)}) collective-permute-start(f32[8,410]{1,0:T(8,128)S(1)} %get-tuple-element.17), channel_id=1, source_target_pairs={{0,1},{1,2},{2,3},{3,4},{4,5},{5,6},{6,7},{7,0},{8,9},{9,10},{10,1... | collective-permute-start | bytes 39368 | tf_op jit(solution)/shard_map/ppermute | solution.py:14
  187.2 5.0 %collective-permute-start.13 = (f32[8,410]{1,0:T(8,128)S(1)}, f32[8,410]{1,0:T(8,128)S(1)}, u32[]{:S(2)}, u32[]{:S(2)}) collective-permute-start(f32[8,410]{1,0:T(8,128)S(1)} %get-tuple-element.18), channel_id=1, source_target_pairs={{0,7},{1,0},{2,1},{3,2},{4,3},{5,4},{6,5},{7,6},{8,15},{9,8},{10,9... | collective-permute-start | bytes 39368 | tf_op jit(solution)/shard_map/ppermute | solution.py:14
where the time goes:
time: 195 us; the launch traced here: 194 us
  local copies, waits for them, and re-layouts  128 us (66%)
  starting transfers between devices  18.2 us (9%)
  other arithmetic  17.6 us (9%)
  matrix products  13.2 us (7%)
  blocking collectives  9.24 us (5%)
  waiting for transfers between devices  6.72 us (3%)
    gather x4, local copies, waits for them, and re-layouts, on_device(): jnp.take(flat_state, wanted, axis=0).reshape(halo_cap, mem_dev, levels)  32.7 us
    gather x1, local copies, waits for them, and re-layouts, on_device(): slot_hweight = jnp.take(horizontal_weight.reshape(-1), inverse_slot, axis=0)  23 us
    unnamed x46, local copies, waits for them, and re-layouts  21.5 us
    ppermute x14, starting transfers between devices, passed_along(): lax.ppermute(x, axis, [(i, (i + by) % devices) for i in range(devices)])  18.2 us
    scatter x1, local copies, waits for them, and re-layouts, on_device(): jnp.zeros((total_slots,), jnp.int32).at[flat_slot].set(slot_ids)  15.5 us
    gather x1, local copies, waits for them, and re-layouts, on_device(): slot_vweight = jnp.take(vertical_weight, slot_obs, axis=0)  12.1 us
    gather x2, local copies, waits for them, and re-layouts, on_device(): jnp.take(flat_state, table[:obs_dev], axis=0)  11.6 us
    dot_general x1, matrix products, on_device(): jnp.dot(equiv, mixing, precision=lax.Precision.HIGHEST, preferred_element...  9.51 us
  transfers between devices with their start and end apart: 14, of which 3 were waited for; matrix products, arithmetic and copies ran while one was open for 72% of the time, Pallas kernels for 0%

commit v1 on v0

--- a/solution.py
+++ b/solution.py
@@ -1,9 +1,14 @@
+import functools
+
 import jax
 import jax.numpy as jnp
 from jax import lax
+from jax.experimental import pallas as pl
+from jax.experimental.pallas import tpu as pltpu
 from jax.sharding import PartitionSpec as P
 
 REG_DEV = 8
+GROUP = 128
 
 
 halo_moves = (-2, -1, 1, 2)
@@ -14,8 +19,54 @@
     return lax.ppermute(x, axis, [(i, (i + by) % devices) for i in range(devices)])
 
 
-def ask_patch(wanted_cells, offset):
-    return passed_along(wanted_cells, "cell", offset)
+def bf16_parts(x, count):
+    parts = []
+    rest = x
+    for _ in range(count):
+        top = lax.reduce_precision(rest, 8, 7)
+        parts.append(top.astype(jnp.bfloat16))
+        rest = rest - top
+    return parts
+
+
+def column_kernel(requests, cell_ref, row_ref, state_ref, weight_ref, out_ref, wide_ref):
+    wide_ref[...] = weight_ref[...].astype(jnp.float32)
+    members = state_ref.shape[1]
+    lane = lax.broadcasted_iota(jnp.int32, (members, GROUP), 1)
+
+    def group(g, carry):
+        first = pl.multiple_of(g * GROUP, GROUP)
+        total = jnp.zeros((members, GROUP), jnp.float32)
+        for j in range(GROUP):
+            column = state_ref[cell_ref[first + j]].astype(jnp.float32)
+            weights = wide_ref[pl.ds(row_ref[first + j], 1), :]
+            dot = jnp.sum(column * weights, axis=1, keepdims=True)
+            total = jnp.where(lane == j, dot, total)
+        out_ref[:, pl.ds(first, GROUP)] = total
+        return carry
+
+    lax.fori_loop(0, requests // GROUP, group, 0)
+
+
+def columns(cell, row, state, weight):
+    requests = cell.shape[0]
+    cells, members, levels = state.shape
+    return pl.pallas_call(
+        functools.partial(column_kernel, requests),
+        out_shape=jax.ShapeDtypeStruct((members, requests), jnp.float32),
+        in_specs=[
+            pl.BlockSpec(memory_space=pltpu.SMEM),
+            pl.BlockSpec(memory_space=pltpu.SMEM),
+            pl.BlockSpec(memory_space=pltpu.VMEM),
+            pl.BlockSpec(memory_space=pltpu.VMEM),
+        ],
+        out_specs=pl.BlockSpec(memory_space=pltpu.VMEM),
+        scratch_shapes=[pltpu.VMEM(weight.shape, jnp.float32)],
+        compiler_params=pltpu.CompilerParams(vmem_limit_bytes=40 * 2**20),
+        cost_estimate=pl.CostEstimate(
+            flops=2 * requests * members * levels, bytes_accessed=2 * state.size, transcendentals=0
+        ),
+    )(cell, row, state, weight)
 
 
 def on_device(
@@ -34,36 +85,56 @@
     obs_dev, neigh = obs_slot.shape
     halo_cap = 3 * obs_dev // 4
     total_slots = 4 * obs_dev
-    flat_state = state.reshape(cell_dev, mem_dev * levels)
-    flat_slot = obs_slot.reshape(-1)
     table = request_cell.reshape(-1)
-    slot_ids = lax.iota(jnp.int32, total_slots)
-    inverse_slot = jnp.zeros((total_slots,), jnp.int32).at[flat_slot].set(slot_ids)
-    slot_obs = inverse_slot // neigh
-    slot_hweight = jnp.take(horizontal_weight.reshape(-1), inverse_slot, axis=0)
-    slot_vweight = jnp.take(vertical_weight, slot_obs, axis=0)
-    own_cols = jnp.take(flat_state, table[:obs_dev], axis=0).reshape(obs_dev, mem_dev, levels)
-    pieces = []
-    pieces.append(
-        jnp.einsum(
-            "rml,rl->mr", own_cols, slot_vweight[:obs_dev], preferred_element_type=jnp.float32
-        )
+    arrived = [passed_along(vertical_weight, "cell", offset) for offset in halo_moves]
+
+    lanes = 128
+    rows = total_slots // lanes
+    slots = obs_slot.T.reshape(-1)
+    hweights = horizontal_weight.T.reshape(-1)
+    obs_of = lax.iota(jnp.int32, total_slots) % obs_dev
+    terms = [(obs_of // 32).astype(jnp.bfloat16), (obs_of % 32).astype(jnp.bfloat16)]
+    terms += bf16_parts(hweights, 3)
+    high = lax.iota(jnp.int32, rows)[:, None] == (slots // lanes)[None, :]
+    low = lax.iota(jnp.int32, lanes)[:, None] == (slots % lanes)[None, :]
+    left = jnp.concatenate(
+        [jnp.where(high, term[None, :], jnp.bfloat16(0)) for term in terms], axis=0
     )
+    by_slot = lax.dot_general(
+        left,
+        low.astype(jnp.bfloat16),
+        (((1,), (1,)), ((), ())),
+        preferred_element_type=jnp.float32,
+    ).reshape(len(terms), total_slots)
+    slot_obs = (by_slot[0] * 32 + by_slot[1] + 0.5).astype(jnp.int32)
+    slot_hweight = by_slot[2] + by_slot[3] + by_slot[4]
+
+    asked = jnp.stack([table, slot_obs])
+    cells_asked = [table[:obs_dev]]
+    rows_asked = [slot_obs[:obs_dev]]
     for number, offset in enumerate(halo_moves):
         lower = obs_dev + number * halo_cap
-        wanted = ask_patch(table[lower : lower + halo_cap], offset)
-        incoming = passed_along(slot_vweight[lower : lower + halo_cap], "cell", offset)
-        picked_cols = jnp.take(flat_state, wanted, axis=0).reshape(halo_cap, mem_dev, levels)
-        at_patch = jnp.einsum(
-            "rml,rl->mr", picked_cols, incoming, preferred_element_type=jnp.float32
-        )
-        pieces.append(passed_along(at_patch, "cell", -offset))
-    equiv = jnp.concatenate(pieces, axis=1)
-    obs_ids = lax.iota(jnp.int32, obs_dev)
-    mixing = (slot_obs[:, None] == obs_ids[None, :]).astype(jnp.float32) * slot_hweight[:, None]
-    own_equiv = jnp.dot(
-        equiv, mixing, precision=lax.Precision.HIGHEST, preferred_element_type=jnp.float32
+        wanted = passed_along(asked[:, lower : lower + halo_cap], "cell", offset)
+        cells_asked.append(wanted[0])
+        rows_asked.append(wanted[1] + (number + 1) * obs_dev)
+    found = columns(
+        jnp.concatenate(cells_asked),
+        jnp.concatenate(rows_asked),
+        state,
+        jnp.concatenate([vertical_weight] + arrived, axis=0),
     )
+    pieces = [found[:, :obs_dev]]
+    for number, offset in enumerate(halo_moves):
+        lower = obs_dev + number * halo_cap
+        pieces.append(passed_along(found[:, lower : lower + halo_cap], "cell", -offset))
+    equiv = jnp.concatenate(pieces, axis=1) * slot_hweight[None, :]
+    mixing = (slot_obs[:, None] == lax.iota(jnp.int32, obs_dev)[None, :]).astype(jnp.bfloat16)
+    own_parts = jnp.dot(
+        jnp.concatenate(bf16_parts(equiv, 3), axis=0),
+        mixing,
+        preferred_element_type=jnp.float32,
+    )
+    own_equiv = own_parts.reshape(3, mem_dev, obs_dev).sum(axis=0)
     everyone = lax.all_gather(own_equiv, "mem", axis=0, tiled=True)
     mean = jnp.mean(everyone, axis=0, keepdims=True)
     spread_all = everyone - mean

time: 195 us -> 86.5 us (0.44)
  local copies, waits for them, and re-layouts: 128 us -> 19 us
  other arithmetic: 17.6 us -> 2.34 us
  Pallas kernels: 0 us -> 12.4 us
  waiting for transfers between devices: 6.72 us -> 13.8 us
  matrix products: 13.2 us -> 7.61 us
  starting transfers between devices: 18.2 us -> 20.6 us
    gather x8 -> x0, local copies, waits for them, and re-layouts: 79.5 us -> none  [the longest x4 32.7 us: on_device(): jnp.take(flat_state, wanted, axis=0).reshape(halo_cap, mem_dev, levels)]
    scatter x1 -> x0, local copies, waits for them, and re-layouts: 15.5 us -> none  [on_device(): jnp.zeros((total_slots,), jnp.int32).at[flat_slot].set(slot_ids)]
    pallas_call x0 -> x1, Pallas kernels: none -> 12.4 us  [columns(): pl.pallas_call(functools.partial(column_kernel, requests), out_shape=jax....]
    select_n x12 -> x1, other arithmetic: 9.93 us -> 0.74 us  [on_device(): low = lax.iota(jnp.int32, lanes)[:, None] == (slots % lanes)[None, :]]
    reshape x3 -> x1, local copies, waits for them, and re-layouts: 8.37 us -> 0.02 us  [on_device(): own_equiv = own_parts.reshape(3, mem_dev, obs_dev).sum(axis=0)]
    dot_general x5 -> x0, other arithmetic: 7.12 us -> none  [the longest x4 4.71 us: on_device(): jnp.einsum('rml,rl->mr', picked_cols, incoming, preferred_element_type=jn...]
    ppermute x14, waiting for transfers between devices: 6.72 us -> 13.8 us  [passed_along(): lax.ppermute(x, axis, [(i, (i + by) % devices) for i in range(devices)])]
    dot_general x1 -> x2, matrix products: 9.51 us -> 3.91 us  [the longest x1 3.39 us: on_device(): jnp.dot(jnp.concatenate(bf16_parts(equiv, 3), axis=0), mixing, preferred_...]
  transfers between devices with their start and end apart: 14 -> 14, of which waited for: 3 -> 6; matrix products, arithmetic and copies ran while one was open for 72% -> 18% of each run, Pallas kernels for 0% -> 0%
where the time goes in v1:
time: 86.5 us; the launch traced here: 85.8 us
  starting transfers between devices  20.6 us (24%)
  local copies, waits for them, and re-layouts  19 us (22%)
  waiting for transfers between devices  13.8 us (16%)
  Pallas kernels  12.4 us (14%)
  blocking collectives  9 us (10%)
  matrix products  7.61 us (9%)
  other arithmetic  2.34 us (3%)
  between operations  1.1 us (1%)
    ppermute x14, starting transfers between devices, passed_along(): lax.ppermute(x, axis, [(i, (i + by) % devices) for i in range(devices)])  20.6 us
    unnamed x30, local copies, waits for them, and re-layouts  17.8 us
    ppermute x14, waiting for transfers between devices, passed_along(): lax.ppermute(x, axis, [(i, (i + by) % devices) for i in range(devices)])  13.8 us
    pallas_call x1, Pallas kernels, columns(): pl.pallas_call(functools.partial(column_kernel, requests), out_shape=jax....  12.4 us
    all_gather x1, blocking collectives, on_device(): everyone = lax.all_gather(own_equiv, 'mem', axis=0, tiled=True)  9 us
    dot_general x1, matrix products, on_device(): jnp.dot(jnp.concatenate(bf16_parts(equiv, 3), axis=0), mixing, preferred_...  3.39 us
    dot_general x1, matrix products, on_device(): jnp.dot(masked, innov, precision=lax.Precision.HIGHEST, preferred_element...  2.75 us
  transfers between devices with their start and end apart: 14, of which 6 were waited for; matrix products, arithmetic and copies ran while one was open for 18% of the time, Pallas kernels for 0%

profile of v1, /device:TPU:0, one launch (start us, length us, event | category | flops | bytes accessed | tf_op | source)
XLA Modules:
  0.0 85.8 jit_solution(10654381854027043964)
XLA Ops:
  0.6 1.1 %copy.28 = bf16[1024,120]{1,0:T(8,128)(2,1)S(1)} copy(bf16[1024,120]{0,1:T(8,128)(2,1)} %param.9) | data formatting | bytes 491520 | tf_op args[1]
  1.7 5.1 %collective-permute-start.4 = (bf16[1024,120]{1,0:T(8,128)(2,1)S(1)}, bf16[1024,120]{1,0:T(8,128)(2,1)S(1)}, u32[]{:S(2)}, u32[]{:S(2)}) collective-permute-start(bf16[1024,120]{1,0:T(8,128)(2,1)S(1)} %copy.28), channel_id=1, source_target_pairs={{0,6},{1,7},{2,0},{3,1},{4,2},{5,3},{6,4},{7,5},{8,14},{9,15},{10,... | collective-permute-start | bytes 737288 | tf_op jit(solution)/shard_map/ppermute | solution.py:19
  6.9 0.5 collective-permute-start.6
  7.4 0.7 collective-permute-start.7
  8.1 0.7 add_select_fusion
  8.8 0.7 fusion.30
  9.5 0.1 fusion.13
  9.6 0.1 fusion.14
  9.7 0.1 fusion.15
  9.7 0.0 copy-start.1
  9.7 0.1 fusion.16
  9.8 0.1 fusion.17
  9.9 0.0 slice-start
  9.9 0.5 fusion.2
  10.4 0.0 copy-done.1
  10.5 3.2 %collective-permute-start = (s32[2,768]{1,0:T(2,128)S(1)}, s32[2,768]{1,0:T(2,128)S(1)}, u32[]{:S(2)}, u32[]{:S(2)}) collective-permute-start(s32[2,768]{1,0:T(2,128)S(1)} %get-tuple-element.28), channel_id=1, source_target_pairs={{0,6},{1,7},{2,0},{3,1},{4,2},{5,3},{6,4},{7,5},{8,14},{9,15},{10,... | collective-permute-start | bytes 18440 | tf_op jit(solution)/shard_map/ppermute | solution.py:19
  13.8 12.4 %copy.29.state_ref = bf16[2048,10,120]{2,1,0:T(8,128)(2,1)} copy(bf16[2048,10,120]{0,2,1:T(8,128)(2,1)} %param.8) | data formatting | bytes 9830400 | tf_op args[0]
  26.2 0.7 collective-permute-start.1
  26.9 1.3 %collective-permute-done.1 = s32[2,768]{1,0:T(2,128)S(1)} collective-permute-done((s32[2,768]{1,0:T(2,128)S(1)}, s32[2,768]{1,0:T(2,128)S(1)}, u32[]{:S(2)}, u32[]{:S(2)}) %collective-permute-start.1) | collective-permute-done | bytes 6176 | tf_op jit(solution)/shard_map/ppermute | solution.py:19
  28.2 1.3 %collective-permute-start.2 = (s32[2,768]{1,0:T(2,128)S(1)}, s32[2,768]{1,0:T(2,128)S(1)}, u32[]{:S(2)}, u32[]{:S(2)}) collective-permute-start(s32[2,768]{1,0:T(2,128)S(1)} %get-tuple-element.26), channel_id=1, source_target_pairs={{0,1},{1,2},{2,3},{3,4},{4,5},{5,6},{6,7},{7,0},{8,9},{9,10},{10,1... | collective-permute-start | bytes 18440 | tf_op jit(solution)/shard_map/ppermute | solution.py:19
  29.5 3.6 %collective-permute-done.2 = s32[2,768]{1,0:T(2,128)S(1)} collective-permute-done((s32[2,768]{1,0:T(2,128)S(1)}, s32[2,768]{1,0:T(2,128)S(1)}, u32[]{:S(2)}, u32[]{:S(2)}) %collective-permute-start.2) | collective-permute-done | bytes 6176 | tf_op jit(solution)/shard_map/ppermute | solution.py:19
  33.1 5.4 %collective-permute-done.3 = s32[2,768]{1,0:T(2,128)S(1)} collective-permute-done((s32[2,768]{1,0:T(2,128)S(1)}, s32[2,768]{1,0:T(2,128)S(1)}, u32[]{:S(2)}, u32[]{:S(2)}) %collective-permute-start.3) | collective-permute-done | bytes 6176 | tf_op jit(solution)/shard_map/ppermute | solution.py:19
  38.8 3.4 %copy-done = bf16[2048,10,120]{2,1,0:T(8,128)(2,1)S(1)} copy-done((bf16[2048,10,120]{2,1,0:T(8,128)(2,1)S(1)}, bf16[2048,10,120]{2,1,0:T(8,128)(2,1)}, u32[]{:S(2)}) %copy-start) | copy-done | bytes 4915224
  42.2 12.4 %shard_map.95 = f32[10,4096]{1,0:T(8,128)S(1)} custom-call(s32[4096]{0:T(1024)S(1)} %constant_dynamic-update-slice_fusion.13.cell_ref, s32[4096]{0:T(1024)S(1)} %constant_dynamic-update-slice_fusion.14.row_ref, bf16[2048,10,120]{2,1,0:T(8,128)(2,1)S(1)} %copy-done, bf16[5120,120]{1,0:T(8,128)(2,1)S(1)} %constant_dynamic-update-slice_fusion.2.weight_ref), custom_call_target="tpu_custom_call" | custom-call | flops 9830400 | bytes 4915200 | tf_op jit(solution)/shard_map/pallas_call | solution.py:54
  54.7 0.1 collective-permute-start.8
  54.7 0.1 collective-permute-start.9
  54.8 3.5 %collective-permute-start.10 = (f32[10,768]{1,0:T(8,128)S(1)}, f32[10,768]{1,0:T(8,128)S(1)}, u32[]{:S(2)}, u32[]{:S(2)}) collective-permute-start(f32[10,768]{1,0:T(8,128)S(1)} %get-tuple-element.18), channel_id=1, source_target_pairs={{0,7},{1,0},{2,1},{3,2},{4,3},{5,4},{6,5},{7,6},{8,15},{9,8},{10,9... | collective-permute-start | bytes 92168 | tf_op jit(solution)/shard_map/ppermute | solution.py:19
  58.3 2.0 %collective-permute-start.11 = (f32[10,768]{1,0:T(8,128)S(1)}, f32[10,768]{1,0:T(8,128)S(1)}, u32[]{:S(2)}, u32[]{:S(2)}) collective-permute-start(f32[10,768]{1,0:T(8,128)S(1)} %get-tuple-element.17), channel_id=1, source_target_pairs={{0,6},{1,7},{2,0},{3,1},{4,2},{5,3},{6,4},{7,5},{8,14},{9,15},{10,... | collective-permute-start | bytes 92168 | tf_op jit(solution)/shard_map/ppermute | solution.py:19
  60.3 0.4 collective-permute-done.8
  60.7 1.7 %collective-permute-done.11 = f32[10,768]{1,0:T(8,128)S(1)} collective-permute-done((f32[10,768]{1,0:T(8,128)S(1)}, f32[10,768]{1,0:T(8,128)S(1)}, u32[]{:S(2)}, u32[]{:S(2)}) %collective-permute-start.11) | collective-permute-done | bytes 30752 | tf_op jit(solution)/shard_map/ppermute | solution.py:19
  62.4 0.1 reduce-precision_convert_fusion.1
  62.5 3.4 %fusion = f32[30,1024]{1,0:T(8,128)S(1)} fusion(s32[4096]{0:T(1024)S(1)} %bitcast.57, bf16[10,4096]{1,0:T(8,128)(2,1)S(1)} %get-tuple-element.15, bf16[10,4096]{1,0:T(8,128)(2,1)S(1)} %get-tuple-element.16, bf16[10,4096]{1,0:T(8,128)(2,1)S(1)} %get-tuple-element.14), kind=kOutput, calls=%fused_computation.1 | convolution fusion | flops 256589824 | bytes 385024 | tf_op jit(solution)/shard_map/dot_general | solution.py:132
  65.9 0.0 copy-start.3
  66.0 9.0 %all-gather = f32[4,10,1024]{2,1,0:T(8,128)S(1)} all-gather(f32[1,10,1024]{2,1,0:T(8,128)S(1)} %bitcast.53), channel_id=1, replica_groups=mesh['mem'=4,'cell'=8] {'mem'}, dimensions={0}, use_global_device_ids=true | all-gather | bytes 204800 | tf_op jit(solution)/shard_map/all_gather | solution.py:138
  75.1 0.2 broadcast_multiply_fusion
  75.3 0.1 mul.70
  75.4 2.7 %fusion.4 = f32[1,24,10]{1,0,2:T(1,128)S(1)} fusion(f32[1024,1,1]{0,1,2:T(1,128)S(1)} %bitcast.60, f32[24,10,1024]{2,1,0:T(8,128)S(1)} %broadcast_multiply_fusion), kind=kOutput, calls=%fused_computation.6 | convolution fusion | flops 2949120 | bytes 988096 | tf_op jit(solution)/shard_map/dot_general | solution.py:158
  78.2 0.1 copy.34
  78.3 0.9 %fusion.23 = f32[240,40]{1,0:T(8,128)S(1)} fusion(f32[240,1024]{1,0:T(8,128)S(1)} %mul.70, f32[40,1024]{1,0:T(8,128)S(1)} %reshape.270, f32[1024]{0:T(1024)S(1)} %get-tuple-element.34, f32[1024]{0:T(1024)S(1)} %get-tuple-element.36), kind=kOutput, calls=%fused_computation.31 | convolution fusion | flops 118046720 | bytes 1193472 | tf_op jit(solution)/shard_map/dot_general | solution.py:151
  79.2 0.1 reshape.267
  79.3 0.1 fusion.33
  79.4 3.5 %collective-permute-start.13 = (f32[8,410]{1,0:T(8,128)S(1)}, f32[8,410]{1,0:T(8,128)S(1)}, u32[]{:S(2)}, u32[]{:S(2)}) collective-permute-start(f32[8,410]{1,0:T(8,128)S(1)} %get-tuple-element.24), channel_id=1, source_target_pairs={{0,7},{1,0},{2,1},{3,2},{4,3},{5,4},{6,5},{7,6},{8,15},{9,8},{10,9... | collective-permute-start | bytes 39368 | tf_op jit(solution)/shard_map/ppermute | solution.py:19
  82.9 1.4 %collective-permute-done.12 = f32[8,410]{1,0:T(8,128)S(1)} collective-permute-done((f32[8,410]{1,0:T(8,128)S(1)}, f32[8,410]{1,0:T(8,128)S(1)}, u32[]{:S(2)}, u32[]{:S(2)}) %collective-permute-start.12) | collective-permute-done | bytes 13152 | tf_op jit(solution)/shard_map/ppermute | solution.py:19
  84.3 0.0 collective-permute-done.13
  84.4 0.1 fusion.36
  84.4 0.7 slice.153
  85.1 0.1 reshape.268
  85.2 0.6 copy.31
  (53 shorter events, 0.6 us)
Async XLA Ops:
  1.7 36.8 %collective-permute-start.4 = (bf16[1024,120]{1,0:T(8,128)(2,1)S(1)}, bf16[1024,120]{1,0:T(8,128)(2,1)S(1)}, u32[]{:S(2)}, u32[]{:S(2)}) collective-permute-start(bf16[1024,120]{1,0:T(8,128)(2,1)S(1)} %copy.28), channel_id=1, source_target_pairs={{0,6},{1,7},{2,0},{3,1},{4,2},{5,3},{6,4},{7,5},{8,14},{9,15},{10,... | collective-permute-start | bytes 737288 | tf_op jit(solution)/shard_map/ppermute | solution.py:19
  6.9 31.8 %collective-permute-start.5 = (bf16[1024,120]{1,0:T(8,128)(2,1)S(1)}, bf16[1024,120]{1,0:T(8,128)(2,1)S(1)}, u32[]{:S(2)}, u32[]{:S(2)}) collective-permute-start(bf16[1024,120]{1,0:T(8,128)(2,1)S(1)} %copy.28), channel_id=1, source_target_pairs={{0,7},{1,0},{2,1},{3,2},{4,3},{5,4},{6,5},{7,6},{8,15},{9,8},{10,9... | collective-permute-start | bytes 737288 | tf_op jit(solution)/shard_map/ppermute | solution.py:19
  6.9 31.8 %collective-permute-start.6 = (bf16[1024,120]{1,0:T(8,128)(2,1)S(1)}, bf16[1024,120]{1,0:T(8,128)(2,1)S(1)}, u32[]{:S(2)}, u32[]{:S(2)}) collective-permute-start(bf16[1024,120]{1,0:T(8,128)(2,1)S(1)} %copy.28), channel_id=1, source_target_pairs={{0,1},{1,2},{2,3},{3,4},{4,5},{5,6},{6,7},{7,0},{8,9},{9,10},{10,1... | collective-permute-start | bytes 737288 | tf_op jit(solution)/shard_map/ppermute | solution.py:19
  7.4 31.4 %collective-permute-start.7 = (bf16[1024,120]{1,0:T(8,128)(2,1)S(1)}, bf16[1024,120]{1,0:T(8,128)(2,1)S(1)}, u32[]{:S(2)}, u32[]{:S(2)}) collective-permute-start(bf16[1024,120]{1,0:T(8,128)(2,1)S(1)} %copy.28), channel_id=1, source_target_pairs={{0,2},{1,3},{2,4},{3,5},{4,6},{5,7},{6,0},{7,1},{8,10},{9,11},{10,... | collective-permute-start | bytes 737288 | tf_op jit(solution)/shard_map/ppermute | solution.py:19
  9.7 0.7 copy-start.1
  9.8 3.8 %copy-start.2 = (s32[1024]{0:T(1024)S(1)}, s32[1024]{0:T(1024)}, u32[]{:S(2)}) copy-start(s32[1024]{0:T(1024)} %param.15) | copy-start | bytes 12292
  9.9 3.9 %slice-start = ((s32[1,4096]{1,0:T(1,128)}), s32[1,1024]{1,0:T(1,128)S(1)}, s32[]{:S(2)}) async-start(s32[1,4096]{1,0:T(1,128)} %param.12), calls=%async_computation | async-start | bytes 8192 | tf_op jit(solution)/shard_map/slice | solution.py:113
  10.5 15.7 %collective-permute-start = (s32[2,768]{1,0:T(2,128)S(1)}, s32[2,768]{1,0:T(2,128)S(1)}, u32[]{:S(2)}, u32[]{:S(2)}) collective-permute-start(s32[2,768]{1,0:T(2,128)S(1)} %get-tuple-element.28), channel_id=1, source_target_pairs={{0,6},{1,7},{2,0},{3,1},{4,2},{5,3},{6,4},{7,5},{8,14},{9,15},{10,... | collective-permute-start | bytes 18440 | tf_op jit(solution)/shard_map/ppermute | solution.py:19
  26.2 2.0 %collective-permute-start.1 = (s32[2,768]{1,0:T(2,128)S(1)}, s32[2,768]{1,0:T(2,128)S(1)}, u32[]{:S(2)}, u32[]{:S(2)}) collective-permute-start(s32[2,768]{1,0:T(2,128)S(1)} %get-tuple-element.27), channel_id=1, source_target_pairs={{0,7},{1,0},{2,1},{3,2},{4,3},{5,4},{6,5},{7,6},{8,15},{9,8},{10,9... | collective-permute-start | bytes 18440 | tf_op jit(solution)/shard_map/ppermute | solution.py:19
  28.2 4.9 %collective-permute-start.2 = (s32[2,768]{1,0:T(2,128)S(1)}, s32[2,768]{1,0:T(2,128)S(1)}, u32[]{:S(2)}, u32[]{:S(2)}) collective-permute-start(s32[2,768]{1,0:T(2,128)S(1)} %get-tuple-element.26), channel_id=1, source_target_pairs={{0,1},{1,2},{2,3},{3,4},{4,5},{5,6},{6,7},{7,0},{8,9},{9,10},{10,1... | collective-permute-start | bytes 18440 | tf_op jit(solution)/shard_map/ppermute | solution.py:19
  33.1 5.4 %collective-permute-start.3 = (s32[2,768]{1,0:T(2,128)S(1)}, s32[2,768]{1,0:T(2,128)S(1)}, u32[]{:S(2)}, u32[]{:S(2)}) collective-permute-start(s32[2,768]{1,0:T(2,128)S(1)} %get-tuple-element.25), channel_id=1, source_target_pairs={{0,2},{1,3},{2,4},{3,5},{4,6},{5,7},{6,0},{7,1},{8,10},{9,11},{10,... | collective-permute-start | bytes 18440 | tf_op jit(solution)/shard_map/ppermute | solution.py:19
  38.8 3.4 %copy-start = (bf16[2048,10,120]{2,1,0:T(8,128)(2,1)S(1)}, bf16[2048,10,120]{2,1,0:T(8,128)(2,1)}, u32[]{:S(2)}) copy-start(bf16[2048,10,120]{2,1,0:T(8,128)(2,1)} %copy.29.state_ref) | copy-start | bytes 14745604
  54.7 6.0 %collective-permute-start.8 = (f32[10,768]{1,0:T(8,128)S(1)}, f32[10,768]{1,0:T(8,128)S(1)}, u32[]{:S(2)}, u32[]{:S(2)}) collective-permute-start(f32[10,768]{1,0:T(8,128)S(1)} %get-tuple-element.20), channel_id=1, source_target_pairs={{0,2},{1,3},{2,4},{3,5},{4,6},{5,7},{6,0},{7,1},{8,10},{9,11},{10,... | collective-permute-start | bytes 92168 | tf_op jit(solution)/shard_map/ppermute | solution.py:19
  54.7 6.0 %collective-permute-start.9 = (f32[10,768]{1,0:T(8,128)S(1)}, f32[10,768]{1,0:T(8,128)S(1)}, u32[]{:S(2)}, u32[]{:S(2)}) collective-permute-start(f32[10,768]{1,0:T(8,128)S(1)} %get-tuple-element.19), channel_id=1, source_target_pairs={{0,1},{1,2},{2,3},{3,4},{4,5},{5,6},{6,7},{7,0},{8,9},{9,10},{10,1... | collective-permute-start | bytes 92168 | tf_op jit(solution)/shard_map/ppermute | solution.py:19
  54.8 5.9 %collective-permute-start.10 = (f32[10,768]{1,0:T(8,128)S(1)}, f32[10,768]{1,0:T(8,128)S(1)}, u32[]{:S(2)}, u32[]{:S(2)}) collective-permute-start(f32[10,768]{1,0:T(8,128)S(1)} %get-tuple-element.18), channel_id=1, source_target_pairs={{0,7},{1,0},{2,1},{3,2},{4,3},{5,4},{6,5},{7,6},{8,15},{9,8},{10,9... | collective-permute-start | bytes 92168 | tf_op jit(solution)/shard_map/ppermute | solution.py:19
  58.3 4.1 %collective-permute-start.11 = (f32[10,768]{1,0:T(8,128)S(1)}, f32[10,768]{1,0:T(8,128)S(1)}, u32[]{:S(2)}, u32[]{:S(2)}) collective-permute-start(f32[10,768]{1,0:T(8,128)S(1)} %get-tuple-element.17), channel_id=1, source_target_pairs={{0,6},{1,7},{2,0},{3,1},{4,2},{5,3},{6,4},{7,5},{8,14},{9,15},{10,... | collective-permute-start | bytes 92168 | tf_op jit(solution)/shard_map/ppermute | solution.py:19
  65.9 9.1 %copy-start.3 = (f32[1024]{0:T(1024)S(1)}, f32[1024]{0:T(1024)}, u32[]{:S(2)}) copy-start(f32[1024]{0:T(1024)} %param.14) | copy-start | bytes 12292
  65.9 9.1 %copy-start.4 = (f32[1024]{0:T(1024)S(1)}, f32[1024]{0:T(1024)}, u32[]{:S(2)}) copy-start(f32[1024]{0:T(1024)} %param.13) | copy-start | bytes 12292
  79.4 5.0 %collective-permute-start.12 = (f32[8,410]{1,0:T(8,128)S(1)}, f32[8,410]{1,0:T(8,128)S(1)}, u32[]{:S(2)}, u32[]{:S(2)}) collective-permute-start(f32[8,410]{1,0:T(8,128)S(1)} %get-tuple-element.23), channel_id=1, source_target_pairs={{0,1},{1,2},{2,3},{3,4},{4,5},{5,6},{6,7},{7,0},{8,9},{9,10},{10,1... | collective-permute-start | bytes 39368 | tf_op jit(solution)/shard_map/ppermute | solution.py:19
  79.4 5.0 %collective-permute-start.13 = (f32[8,410]{1,0:T(8,128)S(1)}, f32[8,410]{1,0:T(8,128)S(1)}, u32[]{:S(2)}, u32[]{:S(2)}) collective-permute-start(f32[8,410]{1,0:T(8,128)S(1)} %get-tuple-element.24), channel_id=1, source_target_pairs={{0,7},{1,0},{2,1},{3,2},{4,3},{5,4},{6,5},{7,6},{8,15},{9,8},{10,9... | collective-permute-start | bytes 39368 | tf_op jit(solution)/shard_map/ppermute | solution.py:19

commit v2 on v1

--- a/solution.py
+++ b/solution.py
@@ -86,7 +86,15 @@
     halo_cap = 3 * obs_dev // 4
     total_slots = 4 * obs_dev
     table = request_cell.reshape(-1)
-    arrived = [passed_along(vertical_weight, "cell", offset) for offset in halo_moves]
+    sharers = lax.axis_size("mem")
+    member = lax.axis_index("mem")
+    part_dev = obs_dev // sharers
+    part = lax.dynamic_slice_in_dim(vertical_weight, member * part_dev, part_dev, 0)
+    mine = jnp.concatenate([passed_along(part, "cell", offset) for offset in halo_moves], axis=0)
+    weight = jnp.concatenate(
+        [mine] + [passed_along(mine, "mem", by) for by in range(1, sharers)] + [vertical_weight],
+        axis=0,
+    )
 
     lanes = 128
     rows = total_slots // lanes
@@ -111,17 +119,20 @@
 
     asked = jnp.stack([table, slot_obs])
     cells_asked = [table[:obs_dev]]
-    rows_asked = [slot_obs[:obs_dev]]
+    rows_asked = [slot_obs[:obs_dev] + len(halo_moves) * obs_dev]
     for number, offset in enumerate(halo_moves):
         lower = obs_dev + number * halo_cap
         wanted = passed_along(asked[:, lower : lower + halo_cap], "cell", offset)
         cells_asked.append(wanted[0])
-        rows_asked.append(wanted[1] + (number + 1) * obs_dev)
+        shift = jnp.mod(member - wanted[1] // part_dev, sharers)
+        rows_asked.append(
+            (shift * len(halo_moves) + number) * part_dev + jnp.mod(wanted[1], part_dev)
+        )
     found = columns(
         jnp.concatenate(cells_asked),
         jnp.concatenate(rows_asked),
         state,
-        jnp.concatenate([vertical_weight] + arrived, axis=0),
+        weight,
     )
     pieces = [found[:, :obs_dev]]
     for number, offset in enumerate(halo_moves):
@@ -135,7 +146,13 @@
         preferred_element_type=jnp.float32,
     )
     own_equiv = own_parts.reshape(3, mem_dev, obs_dev).sum(axis=0)
-    everyone = lax.all_gather(own_equiv, "mem", axis=0, tiled=True)
+    everyone = jnp.zeros((sharers, mem_dev, obs_dev), jnp.float32)
+    everyone = lax.dynamic_update_index_in_dim(everyone, own_equiv, member, 0)
+    for by in range(1, sharers):
+        everyone = lax.dynamic_update_index_in_dim(
+            everyone, passed_along(own_equiv, "mem", by), jnp.mod(member - by, sharers), 0
+        )
+    everyone = everyone.reshape(sharers * mem_dev, obs_dev)
     mean = jnp.mean(everyone, axis=0, keepdims=True)
     spread_all = everyone - mean
     spread_own = own_equiv - mean

time: 86.5 us -> 95.5 us (1.10)
  blocking collectives: 9 us -> 0 us
  starting transfers between devices: 20.6 us -> 29.5 us
  waiting for transfers between devices: 13.8 us -> 22.7 us
    all_gather x1 -> x0, blocking collectives: 9 us -> none  [on_device(): everyone = lax.all_gather(own_equiv, 'mem', axis=0, tiled=True)]
    ppermute x14 -> x20, starting transfers between devices: 20.6 us -> 29.5 us  [passed_along(): lax.ppermute(x, axis, [(i, (i + by) % devices) for i in range(devices)])]
    ppermute x14 -> x20, waiting for transfers between devices: 13.8 us -> 22.7 us  [passed_along(): lax.ppermute(x, axis, [(i, (i + by) % devices) for i in range(devices)])]
    unnamed x30 -> x27, local copies, waits for them, and re-layouts: 17.8 us -> 17.8 us
  transfers between devices with their start and end apart: 14 -> 20, of which waited for: 6 -> 12; matrix products, arithmetic and copies ran while one was open for 18% -> 16% of each run, Pallas kernels for 0% -> 0%
where the time goes in v2:
time: 95.5 us; the launch traced here: 94.9 us
  starting transfers between devices  29.5 us (31%)
  waiting for transfers between devices  22.7 us (24%)
  local copies, waits for them, and re-layouts  19.1 us (20%)
  Pallas kernels  12.4 us (13%)
  matrix products  7.58 us (8%)
  other arithmetic  2.41 us (3%)
  between operations  1.14 us (1%)
    ppermute x20, starting transfers between devices, passed_along(): lax.ppermute(x, axis, [(i, (i + by) % devices) for i in range(devices)])  29.5 us
    ppermute x20, waiting for transfers between devices, passed_along(): lax.ppermute(x, axis, [(i, (i + by) % devices) for i in range(devices)])  22.7 us
    unnamed x27, local copies, waits for them, and re-layouts  17.8 us
    pallas_call x1, Pallas kernels, columns(): pl.pallas_call(functools.partial(column_kernel, requests), out_shape=jax....  12.4 us
    dot_general x1, matrix products, on_device(): jnp.dot(jnp.concatenate(bf16_parts(equiv, 3), axis=0), mixing, preferred_...  3.39 us
    dot_general x1, matrix products, on_device(): jnp.dot(masked, innov, precision=lax.Precision.HIGHEST, preferred_element...  2.75 us
  transfers between devices with their start and end apart: 20, of which 12 were waited for; matrix products, arithmetic and copies ran while one was open for 16% of the time, Pallas kernels for 0%

profile of v2, /device:TPU:0, one launch (start us, length us, event | category | flops | bytes accessed | tf_op | source)
XLA Modules:
  0.0 94.9 jit_solution(16939491841057325941)
XLA Ops:
  0.6 1.1 %copy.13 = bf16[1024,120]{1,0:T(8,128)(2,1)S(1)} copy(bf16[1024,120]{0,1:T(8,128)(2,1)} %param.9) | data formatting | bytes 491520 | tf_op args[1]
  1.8 5.1 %collective-permute-start.4 = (bf16[256,120]{1,0:T(8,128)(2,1)S(1)}, bf16[256,120]{1,0:T(8,128)(2,1)S(1)}, u32[]{:S(2)}, u32[]{:S(2)}) collective-permute-start(bf16[256,120]{1,0:T(8,128)(2,1)S(1)} %constant_dynamic-slice_fusion), channel_id=1, source_target_pairs={{0,6},{1,7},{2,0},{3,1},{4,2},{5,3},{6,4},{7,5},{8,14},{9,15},{10,... | collective-permute-start | bytes 184328 | tf_op jit(solution)/shard_map/ppermute | solution.py:19
  6.9 0.5 collective-permute-start.6
  7.4 0.7 collective-permute-start.7
  8.1 0.7 add_select_fusion
  8.8 0.7 fusion.25
  9.9 0.5 fusion.2
  10.5 3.2 %collective-permute-start = (s32[2,768]{1,0:T(2,128)S(1)}, s32[2,768]{1,0:T(2,128)S(1)}, u32[]{:S(2)}, u32[]{:S(2)}) collective-permute-start(s32[2,768]{1,0:T(2,128)S(1)} %get-tuple-element.34), channel_id=1, source_target_pairs={{0,6},{1,7},{2,0},{3,1},{4,2},{5,3},{6,4},{7,5},{8,14},{9,15},{10,... | collective-permute-start | bytes 18440 | tf_op jit(solution)/shard_map/ppermute | solution.py:19
  13.8 12.4 %copy.15.state_ref = bf16[2048,10,120]{2,1,0:T(8,128)(2,1)} copy(bf16[2048,10,120]{0,2,1:T(8,128)(2,1)} %param.8) | data formatting | bytes 9830400 | tf_op args[0]
  26.2 0.7 collective-permute-start.1
  27.0 1.3 %collective-permute-done.1 = s32[2,768]{1,0:T(2,128)S(1)} collective-permute-done((s32[2,768]{1,0:T(2,128)S(1)}, s32[2,768]{1,0:T(2,128)S(1)}, u32[]{:S(2)}, u32[]{:S(2)}) %collective-permute-start.1) | collective-permute-done | bytes 6176 | tf_op jit(solution)/shard_map/ppermute | solution.py:19
  28.3 1.3 %collective-permute-start.2 = (s32[2,768]{1,0:T(2,128)S(1)}, s32[2,768]{1,0:T(2,128)S(1)}, u32[]{:S(2)}, u32[]{:S(2)}) collective-permute-start(s32[2,768]{1,0:T(2,128)S(1)} %get-tuple-element.32), channel_id=1, source_target_pairs={{0,1},{1,2},{2,3},{3,4},{4,5},{5,6},{6,7},{7,0},{8,9},{9,10},{10,1... | collective-permute-start | bytes 18440 | tf_op jit(solution)/shard_map/ppermute | solution.py:19
  29.6 3.5 %collective-permute-done.2 = s32[2,768]{1,0:T(2,128)S(1)} collective-permute-done((s32[2,768]{1,0:T(2,128)S(1)}, s32[2,768]{1,0:T(2,128)S(1)}, u32[]{:S(2)}, u32[]{:S(2)}) %collective-permute-start.2) | collective-permute-done | bytes 6176 | tf_op jit(solution)/shard_map/ppermute | solution.py:19
  33.2 5.4 %collective-permute-done.3 = s32[2,768]{1,0:T(2,128)S(1)} collective-permute-done((s32[2,768]{1,0:T(2,128)S(1)}, s32[2,768]{1,0:T(2,128)S(1)}, u32[]{:S(2)}, u32[]{:S(2)}) %collective-permute-start.3) | collective-permute-done | bytes 6176 | tf_op jit(solution)/shard_map/ppermute | solution.py:19
  38.8 1.5 %collective-permute-start.8 = (bf16[1024,120]{1,0:T(8,128)(2,1)S(1)}, bf16[1024,120]{1,0:T(8,128)(2,1)S(1)}, u32[]{:S(2)}, u32[]{:S(2)}) collective-permute-start(bf16[1024,120]{1,0:T(8,128)(2,1)S(1)} %get-tuple-element.21), channel_id=1, source_target_pairs={{0,8},{8,16},{16,24},{24,0},{1,9},{9,17},{17,25},{25,1},{2,10},{10... | collective-permute-start | bytes 737288 | tf_op jit(solution)/shard_map/ppermute | solution.py:19
  40.3 1.5 %collective-permute-start.9 = (bf16[1024,120]{1,0:T(8,128)(2,1)S(1)}, bf16[1024,120]{1,0:T(8,128)(2,1)S(1)}, u32[]{:S(2)}, u32[]{:S(2)}) collective-permute-start(bf16[1024,120]{1,0:T(8,128)(2,1)S(1)} %get-tuple-element.21), channel_id=1, source_target_pairs={{0,16},{8,24},{16,0},{24,8},{1,17},{9,25},{17,1},{25,9},{2,18},{10... | collective-permute-start | bytes 737288 | tf_op jit(solution)/shard_map/ppermute | solution.py:19
  41.8 1.4 %collective-permute-start.10 = (bf16[1024,120]{1,0:T(8,128)(2,1)S(1)}, bf16[1024,120]{1,0:T(8,128)(2,1)S(1)}, u32[]{:S(2)}, u32[]{:S(2)}) collective-permute-start(bf16[1024,120]{1,0:T(8,128)(2,1)S(1)} %get-tuple-element.21), channel_id=1, source_target_pairs={{0,24},{8,0},{16,8},{24,16},{1,25},{9,1},{17,9},{25,17},{2,26},{10... | collective-permute-start | bytes 737288 | tf_op jit(solution)/shard_map/ppermute | solution.py:19
  43.3 4.0 %collective-permute-done.8 = bf16[1024,120]{1,0:T(8,128)(2,1)S(1)} collective-permute-done((bf16[1024,120]{1,0:T(8,128)(2,1)S(1)}, bf16[1024,120]{1,0:T(8,128)(2,1)S(1)}, u32[]{:S(2)}, u32[]{:S(2)}) %collective-permute-start.8) | collective-permute-done | bytes 245792 | tf_op jit(solution)/shard_map/ppermute | solution.py:19
  47.3 2.6 %collective-permute-done.9 = bf16[1024,120]{1,0:T(8,128)(2,1)S(1)} collective-permute-done((bf16[1024,120]{1,0:T(8,128)(2,1)S(1)}, bf16[1024,120]{1,0:T(8,128)(2,1)S(1)}, u32[]{:S(2)}, u32[]{:S(2)}) %collective-permute-start.9) | collective-permute-done | bytes 245792 | tf_op jit(solution)/shard_map/ppermute | solution.py:19
  50.0 0.1 collective-permute-done.10
  50.2 3.4 %copy-done = bf16[2048,10,120]{2,1,0:T(8,128)(2,1)S(1)} copy-done((bf16[2048,10,120]{2,1,0:T(8,128)(2,1)S(1)}, bf16[2048,10,120]{2,1,0:T(8,128)(2,1)}, u32[]{:S(2)}) %copy-start) | copy-done | bytes 4915224
  53.6 12.4 %shard_map.95 = f32[10,4096]{1,0:T(8,128)S(1)} custom-call(s32[4096]{0:T(1024)S(1)} %constant_dynamic-update-slice_fusion.20.cell_ref, s32[4096]{0:T(1024)S(1)} %constant_dynamic-update-slice_fusion.21.row_ref, bf16[2048,10,120]{2,1,0:T(8,128)(2,1)S(1)} %copy-done, bf16[5120,120]{1,0:T(8,128)(2,1)S(1)} %constant_dynamic-update-slice_fusion.6.weight_ref), custom_call_target="tpu_custom_call" | custom-call | flops 9830400 | bytes 4915200 | tf_op jit(solution)/shard_map/pallas_call | solution.py:54
  66.0 0.1 collective-permute-start.11
  66.2 3.5 %collective-permute-start.13 = (f32[10,768]{1,0:T(8,128)S(1)}, f32[10,768]{1,0:T(8,128)S(1)}, u32[]{:S(2)}, u32[]{:S(2)}) collective-permute-start(f32[10,768]{1,0:T(8,128)S(1)} %get-tuple-element.16), channel_id=1, source_target_pairs={{0,7},{1,0},{2,1},{3,2},{4,3},{5,4},{6,5},{7,6},{8,15},{9,8},{10,9... | collective-permute-start | bytes 92168 | tf_op jit(solution)/shard_map/ppermute | solution.py:19
  69.7 2.0 %collective-permute-start.14 = (f32[10,768]{1,0:T(8,128)S(1)}, f32[10,768]{1,0:T(8,128)S(1)}, u32[]{:S(2)}, u32[]{:S(2)}) collective-permute-start(f32[10,768]{1,0:T(8,128)S(1)} %get-tuple-element.15), channel_id=1, source_target_pairs={{0,6},{1,7},{2,0},{3,1},{4,2},{5,3},{6,4},{7,5},{8,14},{9,15},{10,... | collective-permute-start | bytes 92168 | tf_op jit(solution)/shard_map/ppermute | solution.py:19
  71.7 0.4 collective-permute-done.11
  72.2 1.6 %collective-permute-done.14 = f32[10,768]{1,0:T(8,128)S(1)} collective-permute-done((f32[10,768]{1,0:T(8,128)S(1)}, f32[10,768]{1,0:T(8,128)S(1)}, u32[]{:S(2)}, u32[]{:S(2)}) %collective-permute-start.14) | collective-permute-done | bytes 30752 | tf_op jit(solution)/shard_map/ppermute | solution.py:19
  73.8 0.1 reduce-precision_convert_fusion.1
  73.9 3.4 %fusion = f32[30,1024]{1,0:T(8,128)S(1)} fusion(s32[4096]{0:T(1024)S(1)} %bitcast.64, bf16[10,4096]{1,0:T(8,128)(2,1)S(1)} %get-tuple-element.13, bf16[10,4096]{1,0:T(8,128)(2,1)S(1)} %get-tuple-element.14, bf16[10,4096]{1,0:T(8,128)(2,1)S(1)} %get-tuple-element.12), kind=kOutput, calls=%fused_computation.1 | convolution fusion | flops 256589824 | bytes 385024 | tf_op jit(solution)/shard_map/dot_general | solution.py:143
  77.4 1.8 %collective-permute-start.15 = (f32[10,1024]{1,0:T(8,128)S(1)}, f32[10,1024]{1,0:T(8,128)S(1)}, u32[]{:S(2)}, u32[]{:S(2)}) collective-permute-start(f32[10,1024]{1,0:T(8,128)S(1)} %reduce_sum.20), channel_id=1, source_target_pairs={{0,8},{8,16},{16,24},{24,0},{1,9},{9,17},{17,25},{25,1},{2,10},{10... | collective-permute-start | bytes 122888 | tf_op jit(solution)/shard_map/ppermute | solution.py:19
  79.2 0.5 collective-permute-start.16
  79.7 2.1 %collective-permute-start.17 = (f32[10,1024]{1,0:T(8,128)S(1)}, f32[10,1024]{1,0:T(8,128)S(1)}, u32[]{:S(2)}, u32[]{:S(2)}) collective-permute-start(f32[10,1024]{1,0:T(8,128)S(1)} %reduce_sum.20), channel_id=1, source_target_pairs={{0,24},{8,0},{16,8},{24,16},{1,25},{9,1},{17,9},{25,17},{2,26},{10... | collective-permute-start | bytes 122888 | tf_op jit(solution)/shard_map/ppermute | solution.py:19
  81.8 0.8 collective-permute-done.15
  82.6 0.9 collective-permute-done.16
  83.5 0.5 collective-permute-done.17
  84.0 0.2 broadcast_multiply_fusion
  84.2 0.1 mul.115
  84.4 2.7 %fusion.4 = f32[1,24,10]{1,0,2:T(1,128)S(1)} fusion(f32[1024,1,1]{0,1,2:T(1,128)S(1)} %bitcast.67, f32[24,10,1024]{2,1,0:T(8,128)S(1)} %broadcast_multiply_fusion), kind=kOutput, calls=%fused_computation.6 | convolution fusion | flops 2949120 | bytes 988096 | tf_op jit(solution)/shard_map/dot_general | solution.py:175
  87.1 0.1 copy.20
  87.3 0.9 fusion.74
  88.2 0.1 reshape.280
  88.3 0.1 fusion.28
  88.4 3.5 %collective-permute-start.19 = (f32[8,410]{1,0:T(8,128)S(1)}, f32[8,410]{1,0:T(8,128)S(1)}, u32[]{:S(2)}, u32[]{:S(2)}) collective-permute-start(f32[8,410]{1,0:T(8,128)S(1)} %get-tuple-element.30), channel_id=1, source_target_pairs={{0,7},{1,0},{2,1},{3,2},{4,3},{5,4},{6,5},{7,6},{8,15},{9,8},{10,9... | collective-permute-start | bytes 39368 | tf_op jit(solution)/shard_map/ppermute | solution.py:19
  92.0 1.4 %collective-permute-done.18 = f32[8,410]{1,0:T(8,128)S(1)} collective-permute-done((f32[8,410]{1,0:T(8,128)S(1)}, f32[8,410]{1,0:T(8,128)S(1)}, u32[]{:S(2)}, u32[]{:S(2)}) %collective-permute-start.18) | collective-permute-done | bytes 13152 | tf_op jit(solution)/shard_map/ppermute | solution.py:19
  93.4 0.1 fusion.31
  93.5 0.7 slice.157
  94.2 0.1 reshape.281
  94.2 0.6 copy.17
  (74 shorter events, 1.2 us)
Async XLA Ops:
  1.8 36.8 %collective-permute-start.4 = (bf16[256,120]{1,0:T(8,128)(2,1)S(1)}, bf16[256,120]{1,0:T(8,128)(2,1)S(1)}, u32[]{:S(2)}, u32[]{:S(2)}) collective-permute-start(bf16[256,120]{1,0:T(8,128)(2,1)S(1)} %constant_dynamic-slice_fusion), channel_id=1, source_target_pairs={{0,6},{1,7},{2,0},{3,1},{4,2},{5,3},{6,4},{7,5},{8,14},{9,15},{10,... | collective-permute-start | bytes 184328 | tf_op jit(solution)/shard_map/ppermute | solution.py:19
  6.9 31.7 %collective-permute-start.5 = (bf16[256,120]{1,0:T(8,128)(2,1)S(1)}, bf16[256,120]{1,0:T(8,128)(2,1)S(1)}, u32[]{:S(2)}, u32[]{:S(2)}) collective-permute-start(bf16[256,120]{1,0:T(8,128)(2,1)S(1)} %constant_dynamic-slice_fusion), channel_id=1, source_target_pairs={{0,7},{1,0},{2,1},{3,2},{4,3},{5,4},{6,5},{7,6},{8,15},{9,8},{10,9... | collective-permute-start | bytes 184328 | tf_op jit(solution)/shard_map/ppermute | solution.py:19
  6.9 31.8 %collective-permute-start.6 = (bf16[256,120]{1,0:T(8,128)(2,1)S(1)}, bf16[256,120]{1,0:T(8,128)(2,1)S(1)}, u32[]{:S(2)}, u32[]{:S(2)}) collective-permute-start(bf16[256,120]{1,0:T(8,128)(2,1)S(1)} %constant_dynamic-slice_fusion), channel_id=1, source_target_pairs={{0,1},{1,2},{2,3},{3,4},{4,5},{5,6},{6,7},{7,0},{8,9},{9,10},{10,1... | collective-permute-start | bytes 184328 | tf_op jit(solution)/shard_map/ppermute | solution.py:19
  7.4 31.3 %collective-permute-start.7 = (bf16[256,120]{1,0:T(8,128)(2,1)S(1)}, bf16[256,120]{1,0:T(8,128)(2,1)S(1)}, u32[]{:S(2)}, u32[]{:S(2)}) collective-permute-start(bf16[256,120]{1,0:T(8,128)(2,1)S(1)} %constant_dynamic-slice_fusion), channel_id=1, source_target_pairs={{0,2},{1,3},{2,4},{3,5},{4,6},{5,7},{6,0},{7,1},{8,10},{9,11},{10,... | collective-permute-start | bytes 184328 | tf_op jit(solution)/shard_map/ppermute | solution.py:19
  9.7 0.7 copy-start.1
  9.8 3.9 %copy-start.2 = (s32[1024]{0:T(1024)S(1)}, s32[1024]{0:T(1024)}, u32[]{:S(2)}) copy-start(s32[1024]{0:T(1024)} %param.15) | copy-start | bytes 12292
  9.8 3.9 %slice-start = ((s32[1,4096]{1,0:T(1,128)}), s32[1,1024]{1,0:T(1,128)S(1)}, s32[]{:S(2)}) async-start(s32[1,4096]{1,0:T(1,128)} %param.12), calls=%async_computation | async-start | bytes 8192 | tf_op jit(solution)/shard_map/slice | solution.py:121
  10.5 15.7 %collective-permute-start = (s32[2,768]{1,0:T(2,128)S(1)}, s32[2,768]{1,0:T(2,128)S(1)}, u32[]{:S(2)}, u32[]{:S(2)}) collective-permute-start(s32[2,768]{1,0:T(2,128)S(1)} %get-tuple-element.34), channel_id=1, source_target_pairs={{0,6},{1,7},{2,0},{3,1},{4,2},{5,3},{6,4},{7,5},{8,14},{9,15},{10,... | collective-permute-start | bytes 18440 | tf_op jit(solution)/shard_map/ppermute | solution.py:19
  26.2 2.0 %collective-permute-start.1 = (s32[2,768]{1,0:T(2,128)S(1)}, s32[2,768]{1,0:T(2,128)S(1)}, u32[]{:S(2)}, u32[]{:S(2)}) collective-permute-start(s32[2,768]{1,0:T(2,128)S(1)} %get-tuple-element.33), channel_id=1, source_target_pairs={{0,7},{1,0},{2,1},{3,2},{4,3},{5,4},{6,5},{7,6},{8,15},{9,8},{10,9... | collective-permute-start | bytes 18440 | tf_op jit(solution)/shard_map/ppermute | solution.py:19
  28.3 4.9 %collective-permute-start.2 = (s32[2,768]{1,0:T(2,128)S(1)}, s32[2,768]{1,0:T(2,128)S(1)}, u32[]{:S(2)}, u32[]{:S(2)}) collective-permute-start(s32[2,768]{1,0:T(2,128)S(1)} %get-tuple-element.32), channel_id=1, source_target_pairs={{0,1},{1,2},{2,3},{3,4},{4,5},{5,6},{6,7},{7,0},{8,9},{9,10},{10,1... | collective-permute-start | bytes 18440 | tf_op jit(solution)/shard_map/ppermute | solution.py:19
  33.1 5.4 %collective-permute-start.3 = (s32[2,768]{1,0:T(2,128)S(1)}, s32[2,768]{1,0:T(2,128)S(1)}, u32[]{:S(2)}, u32[]{:S(2)}) collective-permute-start(s32[2,768]{1,0:T(2,128)S(1)} %get-tuple-element.31), channel_id=1, source_target_pairs={{0,2},{1,3},{2,4},{3,5},{4,6},{5,7},{6,0},{7,1},{8,10},{9,11},{10,... | collective-permute-start | bytes 18440 | tf_op jit(solution)/shard_map/ppermute | solution.py:19
  38.8 8.5 %collective-permute-start.8 = (bf16[1024,120]{1,0:T(8,128)(2,1)S(1)}, bf16[1024,120]{1,0:T(8,128)(2,1)S(1)}, u32[]{:S(2)}, u32[]{:S(2)}) collective-permute-start(bf16[1024,120]{1,0:T(8,128)(2,1)S(1)} %get-tuple-element.21), channel_id=1, source_target_pairs={{0,8},{8,16},{16,24},{24,0},{1,9},{9,17},{17,25},{25,1},{2,10},{10... | collective-permute-start | bytes 737288 | tf_op jit(solution)/shard_map/ppermute | solution.py:19
  40.3 9.7 %collective-permute-start.9 = (bf16[1024,120]{1,0:T(8,128)(2,1)S(1)}, bf16[1024,120]{1,0:T(8,128)(2,1)S(1)}, u32[]{:S(2)}, u32[]{:S(2)}) collective-permute-start(bf16[1024,120]{1,0:T(8,128)(2,1)S(1)} %get-tuple-element.21), channel_id=1, source_target_pairs={{0,16},{8,24},{16,0},{24,8},{1,17},{9,25},{17,1},{25,9},{2,18},{10... | collective-permute-start | bytes 737288 | tf_op jit(solution)/shard_map/ppermute | solution.py:19
  41.8 8.3 %collective-permute-start.10 = (bf16[1024,120]{1,0:T(8,128)(2,1)S(1)}, bf16[1024,120]{1,0:T(8,128)(2,1)S(1)}, u32[]{:S(2)}, u32[]{:S(2)}) collective-permute-start(bf16[1024,120]{1,0:T(8,128)(2,1)S(1)} %get-tuple-element.21), channel_id=1, source_target_pairs={{0,24},{8,0},{16,8},{24,16},{1,25},{9,1},{17,9},{25,17},{2,26},{10... | collective-permute-start | bytes 737288 | tf_op jit(solution)/shard_map/ppermute | solution.py:19
  50.2 3.4 %copy-start = (bf16[2048,10,120]{2,1,0:T(8,128)(2,1)S(1)}, bf16[2048,10,120]{2,1,0:T(8,128)(2,1)}, u32[]{:S(2)}) copy-start(bf16[2048,10,120]{2,1,0:T(8,128)(2,1)} %copy.15.state_ref) | copy-start | bytes 14745604
  66.0 6.1 %collective-permute-start.11 = (f32[10,768]{1,0:T(8,128)S(1)}, f32[10,768]{1,0:T(8,128)S(1)}, u32[]{:S(2)}, u32[]{:S(2)}) collective-permute-start(f32[10,768]{1,0:T(8,128)S(1)} %get-tuple-element.18), channel_id=1, source_target_pairs={{0,2},{1,3},{2,4},{3,5},{4,6},{5,7},{6,0},{7,1},{8,10},{9,11},{10,... | collective-permute-start | bytes 92168 | tf_op jit(solution)/shard_map/ppermute | solution.py:19
  66.1 6.0 %collective-permute-start.12 = (f32[10,768]{1,0:T(8,128)S(1)}, f32[10,768]{1,0:T(8,128)S(1)}, u32[]{:S(2)}, u32[]{:S(2)}) collective-permute-start(f32[10,768]{1,0:T(8,128)S(1)} %get-tuple-element.17), channel_id=1, source_target_pairs={{0,1},{1,2},{2,3},{3,4},{4,5},{5,6},{6,7},{7,0},{8,9},{9,10},{10,1... | collective-permute-start | bytes 92168 | tf_op jit(solution)/shard_map/ppermute | solution.py:19
  66.2 6.0 %collective-permute-start.13 = (f32[10,768]{1,0:T(8,128)S(1)}, f32[10,768]{1,0:T(8,128)S(1)}, u32[]{:S(2)}, u32[]{:S(2)}) collective-permute-start(f32[10,768]{1,0:T(8,128)S(1)} %get-tuple-element.16), channel_id=1, source_target_pairs={{0,7},{1,0},{2,1},{3,2},{4,3},{5,4},{6,5},{7,6},{8,15},{9,8},{10,9... | collective-permute-start | bytes 92168 | tf_op jit(solution)/shard_map/ppermute | solution.py:19
  69.7 4.1 %collective-permute-start.14 = (f32[10,768]{1,0:T(8,128)S(1)}, f32[10,768]{1,0:T(8,128)S(1)}, u32[]{:S(2)}, u32[]{:S(2)}) collective-permute-start(f32[10,768]{1,0:T(8,128)S(1)} %get-tuple-element.15), channel_id=1, source_target_pairs={{0,6},{1,7},{2,0},{3,1},{4,2},{5,3},{6,4},{7,5},{8,14},{9,15},{10,... | collective-permute-start | bytes 92168 | tf_op jit(solution)/shard_map/ppermute | solution.py:19
  77.3 6.7 %copy-start.3 = (f32[1024]{0:T(1024)S(1)}, f32[1024]{0:T(1024)}, u32[]{:S(2)}) copy-start(f32[1024]{0:T(1024)} %param.14) | copy-start | bytes 12292
  77.3 6.7 %copy-start.4 = (f32[1024]{0:T(1024)S(1)}, f32[1024]{0:T(1024)}, u32[]{:S(2)}) copy-start(f32[1024]{0:T(1024)} %param.13) | copy-start | bytes 12292
  77.4 5.2 %collective-permute-start.15 = (f32[10,1024]{1,0:T(8,128)S(1)}, f32[10,1024]{1,0:T(8,128)S(1)}, u32[]{:S(2)}, u32[]{:S(2)}) collective-permute-start(f32[10,1024]{1,0:T(8,128)S(1)} %reduce_sum.20), channel_id=1, source_target_pairs={{0,8},{8,16},{16,24},{24,0},{1,9},{9,17},{17,25},{25,1},{2,10},{10... | collective-permute-start | bytes 122888 | tf_op jit(solution)/shard_map/ppermute | solution.py:19
  79.2 4.3 %collective-permute-start.16 = (f32[10,1024]{1,0:T(8,128)S(1)}, f32[10,1024]{1,0:T(8,128)S(1)}, u32[]{:S(2)}, u32[]{:S(2)}) collective-permute-start(f32[10,1024]{1,0:T(8,128)S(1)} %reduce_sum.20), channel_id=1, source_target_pairs={{0,16},{8,24},{16,0},{24,8},{1,17},{9,25},{17,1},{25,9},{2,18},{10... | collective-permute-start | bytes 122888 | tf_op jit(solution)/shard_map/ppermute | solution.py:19
  79.7 4.3 %collective-permute-start.17 = (f32[10,1024]{1,0:T(8,128)S(1)}, f32[10,1024]{1,0:T(8,128)S(1)}, u32[]{:S(2)}, u32[]{:S(2)}) collective-permute-start(f32[10,1024]{1,0:T(8,128)S(1)} %reduce_sum.20), channel_id=1, source_target_pairs={{0,24},{8,0},{16,8},{24,16},{1,25},{9,1},{17,9},{25,17},{2,26},{10... | collective-permute-start | bytes 122888 | tf_op jit(solution)/shard_map/ppermute | solution.py:19
  88.4 5.0 %collective-permute-start.18 = (f32[8,410]{1,0:T(8,128)S(1)}, f32[8,410]{1,0:T(8,128)S(1)}, u32[]{:S(2)}, u32[]{:S(2)}) collective-permute-start(f32[8,410]{1,0:T(8,128)S(1)} %get-tuple-element.29), channel_id=1, source_target_pairs={{0,1},{1,2},{2,3},{3,4},{4,5},{5,6},{6,7},{7,0},{8,9},{9,10},{10,1... | collective-permute-start | bytes 39368 | tf_op jit(solution)/shard_map/ppermute | solution.py:19
  88.4 5.0 %collective-permute-start.19 = (f32[8,410]{1,0:T(8,128)S(1)}, f32[8,410]{1,0:T(8,128)S(1)}, u32[]{:S(2)}, u32[]{:S(2)}) collective-permute-start(f32[8,410]{1,0:T(8,128)S(1)} %get-tuple-element.30), channel_id=1, source_target_pairs={{0,7},{1,0},{2,1},{3,2},{4,3},{5,4},{6,5},{7,6},{8,15},{9,8},{10,9... | collective-permute-start | bytes 39368 | tf_op jit(solution)/shard_map/ppermute | solution.py:19
